TPU v7x, 128 devices: a whole 4x4x4 slice. The times are simulated.
128 devices in a mesh: row: 2 (over x_lo), circ: 16 (over z, y), rad: 4 (over x_hi, core).
Axes of the slice: x: 4 (x_hi: 2, x_lo: 2; x = x_hi * 2 + x_lo), y: 4, z: 4, core: 2. Of those that a mesh axis runs over, the one named last changes fastest.
Arguments:
- state: float32 [2, 5, 512, 64, 512], P('row', None, 'circ', 'rad'), as said below
- time_source: float32 [2, 5, 512, 64, 512], P('row', None, 'circ', 'rad'), may hold values from -3 to 3
- pseudo_step: float32 [2, 512, 64, 512], P('row', 'circ', 'rad'), may hold values from 0.05 to 0.5
- offsets: int32 [64], P('rad'), may hold values from 0 to 511
- weights: float32 [64], P('rad'), may hold values from 0 to 1
Outputs:
- increment: float32 [2, 5, 512, 64, 512], P('row', None, 'circ', 'rad')
Inputs may be any that keep to these rules, and one draw needn't show every extreme that they name: In every cell the density lies between 0.5 and 1.5 and the pressure computed from the state between 0.6 and 1.1.
All inputs are finite; a program needn't handle non-finite values.
Results may differ from a plain program's by a relative error of at most 0.000057.
Values sent between devices are 32-bit elements; how exact they have to be, the bound alone decides.
No kernel may reach another device: no remote copies, remote signals or barrier semaphores. Data moves between devices by JAX's collectives and lax.ppermute only.
A program may use at most 128 MiB of HBM per device.

v0:
```python
import jax
import jax.numpy as jnp
import numpy as np
from jax import lax
from jax.sharding import PartitionSpec as P

SWEEPS = 2


GAMMA = 1.4
GAMMA_LESS = 0.4
SECOND_COEF = 0.5
FOURTH_COEF = 0.03125
RATE = 0.75
GRID_SPEED = 0.5
AXIAL_COUPLING = 0.8
CIRC_COUPLING = 0.6
RADIAL_COUPLING = 0.6


def partner(value, axis, stride):
    mask = 2**stride
    pairs = [(source, source ^ mask) for source in range(lax.axis_size(axis))]
    return lax.ppermute(value, axis, pairs)


def copy_for_each(x, axis):
    peers = lax.axis_size(axis)
    return lax.all_to_all(jnp.broadcast_to(x[None], (peers, *x.shape)), axis, 0, 0, tiled=True)


def laid_out(parts, dim):
    parts = jnp.moveaxis(parts, 0, dim)
    shape = parts.shape
    return parts.reshape(*shape[:dim], shape[dim] * shape[dim + 1], *shape[dim + 2 :])


def gathered_copies(x, axis, dim):
    parts = copy_for_each(x, axis)
    return laid_out(parts, dim)


def with_halo(x, sides, width):
    edges = {}
    for axis, dim in sides:
        peers, length = (lax.axis_size(axis), x.shape[dim])
        up = [(i, (i + 1) % peers) for i in range(peers)]
        last = lax.slice_in_dim(x, length - width, length, axis=dim)
        initial = lax.slice_in_dim(x, 0, width, axis=dim)
        edges[dim] = (
            lax.ppermute(last, axis, up),
            lax.ppermute(initial, axis, [(b, a) for a, b in up]),
        )
    done = []
    for _, dim in sides:
        low, high = edges[dim]
        around = [(width, width) if d in done else (0, 0) for d in range(x.ndim)]
        x = jnp.concatenate([jnp.pad(low, around), x, jnp.pad(high, around)], axis=dim)
        done.append(dim)
    return x


def padded(block, sides, width):
    for axis, dim in sides:
        count = lax.axis_size(axis)
        forward = [(i, i + 1) for i in range(count - 1)]
        forward.append((count - 1, 0))
        backward = [(target, source) for source, target in forward]
        low = lax.ppermute(
            lax.slice_in_dim(block, block.shape[dim] - width, None, axis=dim), axis, forward
        )
        high = lax.ppermute(lax.slice_in_dim(block, 0, width, axis=dim), axis, backward)
        block = jnp.concatenate([low, block, high], axis=dim)
    return block


def axial_table(length):
    modes_index = np.arange(1, length + 1) * 1.0
    angle = np.pi / (length + 1)
    modes = np.sin(np.outer(modes_index, modes_index) * angle)
    eigen = 1.0 + 2.0 * AXIAL_COUPLING - 2.0 * AXIAL_COUPLING * np.cos(modes_index * angle)
    return modes / eigen[None, :] @ modes.T * (2.0 / (length + 1))


def slab_cut(field, start_at, length, direction):
    return lax.slice_in_dim(field, start_at, start_at + length, axis=direction)


def flux_balance(margin, direction, component, grid_speed):
    length = margin.shape[direction] - 4
    density = margin[0]
    velocity = margin[1:4] / density
    pressure = GAMMA_LESS * (
        margin[4]
        - 0.5
        * density
        * (velocity[0] * velocity[0] + velocity[1] * velocity[1] + velocity[2] * velocity[2])
    )
    normal = velocity[component - 1]
    relative = normal - grid_speed
    radius = jnp.abs(relative) + jnp.sqrt(GAMMA * pressure / density)
    fluxes = margin * relative
    fluxes = fluxes.at[component].add(pressure)
    fluxes = fluxes.at[4].add(pressure * normal)
    upper_p = slab_cut(pressure, 2, length + 2, direction)
    middle_p = slab_cut(pressure, 1, length + 2, direction)
    lower_p = slab_cut(pressure, 0, length + 2, direction)
    sensor = jnp.abs(upper_p - 2.0 * middle_p + lower_p) / (upper_p + 2.0 * middle_p + lower_p)
    second_coef = SECOND_COEF * jnp.maximum(
        slab_cut(sensor, 0, length + 1, direction), slab_cut(sensor, 1, length + 1, direction)
    )
    fourth_coef = jnp.maximum(0.0, FOURTH_COEF - second_coef)
    face_speed = 0.5 * (
        slab_cut(radius, 1, length + 1, direction) + slab_cut(radius, 2, length + 1, direction)
    )
    before_cell = slab_cut(margin, 0, length + 1, direction)
    near_cell = slab_cut(margin, 1, length + 1, direction)
    far_cell = slab_cut(margin, 2, length + 1, direction)
    beyond_cell = slab_cut(margin, 3, length + 1, direction)
    first_jump = far_cell - near_cell
    third_jump = beyond_cell - 3.0 * far_cell + 3.0 * near_cell - before_cell
    face_flux = 0.5 * (
        slab_cut(fluxes, 1, length + 1, direction) + slab_cut(fluxes, 2, length + 1, direction)
    ) - face_speed * (second_coef * first_jump - fourth_coef * third_jump)
    return slab_cut(face_flux, 1, length, direction) - slab_cut(face_flux, 0, length, direction)


def jacobi(field, direction, coupling):
    length = field.shape[direction] - 2
    centre = slab_cut(field, 1, length, direction)
    return (
        centre
        + coupling * (slab_cut(field, 2, length, direction) + slab_cut(field, 0, length, direction))
    ) / (1.0 + 2.0 * coupling)


def wall_zero(field, width, first_rad, last_rad):
    extent = field.shape[2]
    position = jnp.arange(extent, dtype=jnp.int32)[None, None, :, None]
    masked = first_rad & (position < width) | last_rad & (position >= extent - width)
    return jnp.where(masked, 0.0, field)


def on_device(state, time_source, pseudo_step, offsets, weights):
    cells = state[0]
    source = time_source[0]
    pseudo = pseudo_step[0]
    count_t = cells.shape[1]
    count_r = cells.shape[2]
    count_a = cells.shape[3]
    total_t = count_t * lax.axis_size("circ")
    rotor = lax.axis_index("row") == 1
    first_rad = lax.axis_index("rad") == 0
    last_rad = lax.axis_index("rad") == lax.axis_size("rad") - 1
    mirror_sign = jnp.array([1.0, 1.0, 1.0, -1.0, 1.0], jnp.float32)[:, None, None, None]
    own_face = jnp.where(rotor, cells[:, :, :, :2], cells[:, :, :, count_a - 2 :])
    moved_face = jnp.transpose(own_face, (3, 0, 2, 1))
    facing_face = partner(moved_face, "row", 0)
    plane_cycle = gathered_copies(facing_face, "circ", 3)
    position = lax.axis_index("circ") * count_t + jnp.arange(count_t, dtype=jnp.int32)[None, :]
    offset_col = offsets[:, None]
    weight_col = weights[:, None]
    lead_index = jnp.where(
        rotor, (position + offset_col) % total_t, (position - offset_col - 1) % total_t
    )
    trail_index = jnp.where(
        rotor, (position + offset_col + 1) % total_t, (position - offset_col) % total_t
    )
    lead_weight = jnp.where(rotor, 1.0 - weight_col, weight_col)
    trail_weight = jnp.where(rotor, weight_col, 1.0 - weight_col)
    full_shape = (2, 5, count_r, count_t)
    lead_cells = jnp.take_along_axis(
        plane_cycle, jnp.broadcast_to(lead_index[None, None], full_shape), axis=3
    )
    trail_cells = jnp.take_along_axis(
        plane_cycle, jnp.broadcast_to(trail_index[None, None], full_shape), axis=3
    )
    picked = lead_weight[None, None] * lead_cells + trail_weight[None, None] * trail_cells
    plane_ghost = jnp.transpose(picked, (1, 3, 2, 0))
    first_edge = jnp.concatenate([cells[:, :, :, :1], cells[:, :, :, :1]], axis=3)
    last_edge = jnp.concatenate(
        [cells[:, :, :, count_a - 1 :], cells[:, :, :, count_a - 1 :]], axis=3
    )
    left_rim = jnp.where(rotor, plane_ghost, first_edge)
    right_rim = jnp.where(rotor, last_edge, plane_ghost)
    axial_margin = jnp.concatenate([left_rim, cells, right_rim], axis=3)
    margin = with_halo(cells, (("circ", 1), ("rad", 2)), 2)
    circ_margin = margin[:, :, 2 : count_r + 2, :]
    radial_part = margin[:, 2 : count_t + 2, :, :]
    lower_rim = jnp.where(
        first_rad, jnp.flip(cells[:, :, 0:2], axis=2) * mirror_sign, radial_part[:, :, 0:2]
    )
    upper_rim = jnp.where(
        last_rad,
        jnp.flip(cells[:, :, count_r - 2 :], axis=2) * mirror_sign,
        radial_part[:, :, count_r + 2 :],
    )
    radial_margin = jnp.concatenate([lower_rim, cells, upper_rim], axis=2)
    grid_speed = GRID_SPEED * lax.axis_index("row").astype(jnp.float32)
    balance = (
        flux_balance(axial_margin, -1, 1, 0.0)
        + flux_balance(circ_margin, -3, 2, grid_speed)
        + flux_balance(radial_margin, -2, 3, 0.0)
    )
    increment_raw = -(pseudo[None] * (balance + RATE * cells + source))
    inverse = jnp.asarray(axial_table(count_a), dtype=jnp.float32)
    smooth = jnp.dot(
        increment_raw.reshape(-1, count_a),
        inverse,
        precision=lax.Precision.HIGHEST,
        preferred_element_type=jnp.float32,
    ).reshape(increment_raw.shape)
    widened = padded(smooth, (("circ", 1), ("rad", 2)), SWEEPS)
    for _ in range(SWEEPS):
        widened = jacobi(widened, -3, CIRC_COUPLING)
    for sweep in range(SWEEPS):
        widened = wall_zero(widened, SWEEPS - sweep, first_rad, last_rad)
        widened = jacobi(widened, -2, RADIAL_COUPLING)
    smooth = widened
    return smooth[None]


def solution(mesh):
    return jax.shard_map(
        on_device,
        mesh=mesh,
        in_specs=(
            P("row", None, "circ", "rad", None),
            P("row", None, "circ", "rad", None),
            P("row", "circ", "rad", None),
            P("rad"),
            P("rad"),
        ),
        out_specs=P("row", None, "circ", "rad", None),
        check_vma=False,
    )
```

profile of v0, /device:TPU:1, one launch (start us, length us, event | category | flops | bytes accessed | tf_op | source)
XLA Modules:
  0.0 329.4 jit_solution(4406436997471591897)
XLA Ops:
  0.0 3.2 fusion.110
  12.6 4.9 %collective-permute-start.2 = (f32[5,2,16,512]{3,2,1,0:T(8,128)}, f32[5,2,16,512]{3,2,1,0:T(8,128)S(1)}, u32[]{:S(2)}, u32[]{:S(2)}) collective-permute-start(f32[5,2,16,512]{3,2,1,0:T(8,128)} %get-tuple-element.100), channel_id=1, source_target_pairs={{4,0},{8,4},{12,8},{16,12},{20,16},{24,20},{28,24},{32,28},{36,32}... | collective-permute-start | bytes 983048 | tf_op jit(solution)/shard_map/ppermute | solution.py:52
  21.5 3.7 %fusion.108 = (f32[5,32,16,1]{3,2,1,0:T(8,128)}, f32[5,32,16,1]{3,2,1,0:T(8,128)}) fusion(f32[5,32,16,512]{3,2,1,0:T(8,128)} %bitcast.121), kind=kLoop, calls=%fused_computation.224 | loop fusion | bytes 40960 | tf_op jit(solution)/shard_map/slice | solution.py:182
  26.9 4.3 %rev.8 = f32[5,32,2,512]{3,2,1,0:T(2,128)} reverse(f32[5,32,2,512]{3,2,1,0:T(2,128)S(1)} %get-tuple-element.103), dimensions={2} | reverse | bytes 1310720 | tf_op jit(solution)/shard_map/jit(_flip)/rev | solution.py:195
  31.2 4.3 %rev.7 = f32[5,32,2,512]{3,2,1,0:T(2,128)} reverse(f32[5,32,2,512]{3,2,1,0:T(2,128)S(1)} %get-tuple-element.102), dimensions={2} | reverse | bytes 1310720 | tf_op jit(solution)/shard_map/jit(_flip)/rev | solution.py:191
  40.5 3.8 %all-to-all-start = ((f32[16,1,5120]{2,1,0:T(1,128)}), f32[16,1,5120]{2,1,0:T(1,128)S(1)}, u32[]{:S(2)}, u32[]{:S(2)}) async-start(f32[16,1,5120]{2,1,0:T(1,128)} %reshape.455), calls=%async_computation | async-start | bytes 655360 | tf_op jit(solution)/shard_map/all_to_all | solution.py:29
  44.3 3.3 pad_maximum_fusion.7
  58.0 59.5 %gather_fusion.1 = f32[5120]{0:T(1024)S(1)} fusion(f32[2,5,16,512]{3,2,1,0:T(8,128)S(1)} %reshape.420, s32[5120]{0:T(1024)S(1)} %reshape.450), kind=kCustom, calls=%fused_computation.1.clone | custom fusion | bytes 122880 | tf_op jit(solution)/shard_map/jit(take_along_axis)/gather | solution.py:175
  119.2 59.5 %gather_fusion = f32[5120]{0:T(1024)S(1)} fusion(f32[2,5,16,512]{3,2,1,0:T(8,128)S(1)} %reshape.420, s32[5120]{0:T(1024)S(1)} %reshape.445), kind=kCustom, calls=%fused_computation.clone | custom fusion | bytes 122880 | tf_op jit(solution)/shard_map/jit(take_along_axis)/gather | solution.py:172
  180.3 4.4 %maximum_select_fusion.1 = (f32[5,32,16,2]{3,2,1,0:T(8,128)S(1)}, f32[5,32,16,2]{3,2,1,0:T(8,128)S(1)}) fusion(f32[5,32,16,1]{3,2,1,0:T(8,128)} %get-tuple-element.98, pred[]{:T(512)S(6)} %eq.16, f32[2,5,16,32]{0,2,3,1:T(8,128)} %copy.167, s32[16,32]{0,1:T(8,128)S(1)} %get-tuple-element.111, s32[16,32]{0,1:T(8,128)S(1)} %get-tuple-element.110, ...), kind=kLoop, calls=%fused_computation.138 | loop fusion | flops 87040 | bytes 111745 | tf_op jit(solution)/shard_map/jit(_where)/select_n | solution.py:185
  184.8 4.6 %pad_maximum_fusion.6 = f32[5,32,16,516]{3,2,1,0:T(8,128)S(1)} fusion(f32[5,32,16,2]{3,2,1,0:T(8,128)S(1)} %get-tuple-element.104, f32[5,32,16,512]{3,2,1,0:T(8,128)} %bitcast.123, f32[5,32,16,2]{3,2,1,0:T(8,128)S(1)} %get-tuple-element.105), kind=kLoop, calls=%fused_computation.44 | loop fusion | flops 2641920 | bytes 10567680 | tf_op jit(solution)/shard_map/concatenate | solution.py:186
  212.3 11.6 %fusion.23 = f32[5,32,16,513]{3,2,1,0:T(8,128)} fusion(f32[5,32,16,512]{3,2,1,0:T(8,128)S(1)} %bitcast.128, f32[5,32,16,2]{3,2,1,0:T(8,128)S(1)} %get-tuple-element.105, f32[5,32,16,2]{3,2,1,0:T(8,128)S(1)} %get-tuple-element.104, f32[5,32,16,516]{3,2,1,0:T(8,128)S(1)} %fusion.72, f32[32,16,513]{2,1,0:T(8,128)S(1)} %get-tuple-element.80, ...), kind=kLoop, calls=%fused_computation.36 | loop fusion | flops 22325760 | bytes 24195072 | tf_op jit(solution)/shard_map/sub | solution.py:122
  224.0 6.3 %fusion.33 = f32[5,33,16,512]{3,2,1,0:T(8,128)} fusion(f32[5,32,16,512]{3,2,1,0:T(8,128)S(1)} %bitcast.129, f32[5,2,16,512]{3,2,1,0:T(8,128)S(1)} %collective-permute-done.1, f32[5,2,16,512]{3,2,1,0:T(8,128)S(1)} %copy-done.14, f32[5,36,16,512]{3,2,1,0:T(8,128)S(1)} %fusion.80, f32[33,16,512]{2,1,0:T(8,128)S(1)} %copy-done.10, ...), kind=kLoop, calls=%fused_computation.57 | loop fusion | flops 22978560 | bytes 25362432 | tf_op jit(solution)/shard_map/sub | solution.py:122
  242.6 8.2 %fusion.15 = f32[5,32,17,512]{3,2,1,0:T(8,128)} fusion(f32[5,32,16,512]{3,2,1,0:T(8,128)S(1)} %bitcast.132, f32[5,32,2,512]{3,2,1,0:T(2,128)S(1)} %get-tuple-element.115, f32[5,32,2,512]{3,2,1,0:T(2,128)S(1)} %get-tuple-element.114, f32[5,32,20,512]{3,2,1,0:T(8,128)S(1)} %fusion.59, f32[32,17,512]{2,1,0:T(8,128)S(1)} %get-tuple-element.90, ...), kind=kLoop, calls=%fused_computation.22 | loop fusion | flops 23674880 | bytes 26607616 | tf_op jit(solution)/shard_map/sub | solution.py:122
  250.9 21.2 %fusion.46 = f32[5,32,16,512]{3,2,1,0:T(8,128)} fusion(f32[512,512,1,1]{1,0,3,2:T(8,128)S(1)} %copy-done.18, f32[5,32,17,512]{3,2,1,0:T(8,128)} %fusion.15, f32[5,33,16,512]{3,2,1,0:T(8,128)} %fusion.33, f32[5,32,16,513]{3,2,1,0:T(8,128)} %fusion.23, f32[1,5,32,16,512]{4,3,2,1,0:T(8,128)} %param.22, f32[32,16,512]{2,1,0:T(8,128)S(1)} %bitcast.136, ...), kind=kOutput, calls=%fused_computation.74 | convolution fusion | flops 8066170880 | bytes 49283072 | tf_op jit(solution)/shard_map/dot_general | solution.py:207
  273.2 4.8 %collective-permute-start.6 = (f32[5,2,16,512]{3,2,1,0:T(8,128)S(1)}, f32[5,2,16,512]{3,2,1,0:T(8,128)S(1)}, u32[]{:S(2)}, u32[]{:S(2)}) collective-permute-start(f32[5,2,16,512]{3,2,1,0:T(8,128)S(1)} %get-tuple-element.97), channel_id=1, source_target_pairs={{4,0},{8,4},{12,8},{16,12},{20,16},{24,20},{28,24},{32,28},{36,32}... | collective-permute-start | bytes 983048 | tf_op jit(solution)/shard_map/ppermute | solution.py:72
  278.3 6.9 %collective-permute-done.6 = f32[5,2,16,512]{3,2,1,0:T(8,128)S(1)} collective-permute-done((f32[5,2,16,512]{3,2,1,0:T(8,128)S(1)}, f32[5,2,16,512]{3,2,1,0:T(8,128)S(1)}, u32[]{:S(2)}, u32[]{:S(2)}) %collective-permute-start.6) | collective-permute-done | bytes 327712 | tf_op jit(solution)/shard_map/ppermute | solution.py:72
  285.2 5.5 %collective-permute-done.5 = f32[5,2,16,512]{3,2,1,0:T(8,128)S(1)} collective-permute-done((f32[5,2,16,512]{3,2,1,0:T(8,128)S(1)}, f32[5,2,16,512]{3,2,1,0:T(8,128)S(1)}, u32[]{:S(2)}, u32[]{:S(2)}) %collective-permute-start.5) | collective-permute-done | bytes 327712 | tf_op jit(solution)/shard_map/ppermute | solution.py:69
  290.6 3.5 %pad_maximum_fusion.12 = (f32[5,36,2,512]{3,2,1,0:T(2,128)S(1)}, f32[5,36,2,512]{3,2,1,0:T(2,128)S(1)}) fusion(f32[5,2,16,512]{3,2,1,0:T(8,128)S(1)} %collective-permute-done.6, f32[5,32,16,512]{3,2,1,0:T(8,128)} %fusion.46, f32[5,2,16,512]{3,2,1,0:T(8,128)S(1)} %collective-permute-done.5), kind=kLoop, calls=%fused_computation.179 | loop fusion | flops 737280 | bytes 7372800 | tf_op jit(solution)/shard_map/slice | solution.py:70
  297.5 14.6 %collective-permute-done.8 = f32[5,36,2,512]{3,2,1,0:T(2,128)S(1)} collective-permute-done((f32[5,36,2,512]{3,2,1,0:T(2,128)S(1)}, f32[5,36,2,512]{3,2,1,0:T(2,128)S(1)}, u32[]{:S(2)}, u32[]{:S(2)}) %collective-permute-start.8) | collective-permute-done | bytes 737312 | tf_op jit(solution)/shard_map/ppermute | solution.py:72
  313.6 3.1 pad_maximum_fusion
  316.8 3.2 fusion.2
  320.0 3.1 fusion.10
  325.7 3.2 fusion.40
  (132 shorter events, 77.6 us)
Async XLA Ops:
  4.2 226.1 %collective-permute-start.4 = (f32[5,32,2,512]{3,1,2,0:T(8,128)}, f32[5,32,2,512]{3,1,2,0:T(8,128)}, u32[]{:S(2)}, u32[]{:S(2)}) collective-permute-start(f32[5,32,2,512]{3,1,2,0:T(8,128)} %copy.170), channel_id=1, source_target_pairs={{1,0},{2,1},{3,2},{0,3},{5,4},{6,5},{7,6},{4,7},{9,8},{10,9},{11,1... | collective-permute-start | bytes 1966088 | tf_op jit(solution)/shard_map/ppermute | solution.py:52
  6.5 223.8 %collective-permute-start.3 = (f32[5,32,2,512]{3,1,2,0:T(8,128)}, f32[5,32,2,512]{3,1,2,0:T(8,128)}, u32[]{:S(2)}, u32[]{:S(2)}) collective-permute-start(f32[5,32,2,512]{3,1,2,0:T(8,128)} %copy.168), channel_id=1, source_target_pairs={{0,1},{1,2},{2,3},{3,0},{4,5},{5,6},{6,7},{7,4},{8,9},{9,10},{10,1... | collective-permute-start | bytes 1966088 | tf_op jit(solution)/shard_map/ppermute | solution.py:51
  11.3 33.0 %collective-permute-start.1 = (f32[5,2,16,512]{3,2,1,0:T(8,128)}, f32[5,2,16,512]{3,2,1,0:T(8,128)S(1)}, u32[]{:S(2)}, u32[]{:S(2)}) collective-permute-start(f32[5,2,16,512]{3,2,1,0:T(8,128)} %get-tuple-element.101), channel_id=1, source_target_pairs={{0,4},{4,8},{8,12},{12,16},{16,20},{20,24},{24,28},{28,32},{32,36}... | collective-permute-start | bytes 983048 | tf_op jit(solution)/shard_map/ppermute | solution.py:51
  12.6 31.7 %collective-permute-start.2 = (f32[5,2,16,512]{3,2,1,0:T(8,128)}, f32[5,2,16,512]{3,2,1,0:T(8,128)S(1)}, u32[]{:S(2)}, u32[]{:S(2)}) collective-permute-start(f32[5,2,16,512]{3,2,1,0:T(8,128)} %get-tuple-element.100), channel_id=1, source_target_pairs={{4,0},{8,4},{12,8},{16,12},{20,16},{24,20},{28,24},{32,28},{36,32}... | collective-permute-start | bytes 983048 | tf_op jit(solution)/shard_map/ppermute | solution.py:52
  20.2 4.9 %copy-start.19 = (s32[16]{0:T(128)S(1)}, s32[16]{0:T(128)}, u32[]{:S(2)}) copy-start(s32[16]{0:T(128)} %param.24) | copy-start | bytes 196
  20.2 17.9 %collective-permute-start = (f32[2,5,16,32]{3,2,1,0:T(8,128)S(1)}, f32[2,5,16,32]{3,2,1,0:T(8,128)}, u32[]{:S(2)}, u32[]{:S(2)}) collective-permute-start(f32[2,5,16,32]{3,2,1,0:T(8,128)S(1)} %copy.162), channel_id=1, source_target_pairs={{0,64},{64,0},{1,65},{65,1},{2,66},{66,2},{3,67},{67,3},{4,68},{68... | collective-permute-start | bytes 61448 | tf_op jit(solution)/shard_map/ppermute | solution.py:24
  40.5 13.8 %all-to-all-start = ((f32[16,1,5120]{2,1,0:T(1,128)}), f32[16,1,5120]{2,1,0:T(1,128)S(1)}, u32[]{:S(2)}, u32[]{:S(2)}) async-start(f32[16,1,5120]{2,1,0:T(1,128)} %reshape.455), calls=%async_computation | async-start | bytes 655360 | tf_op jit(solution)/shard_map/all_to_all | solution.py:29
  189.5 5.9 %slice-start = ((s8[5242880]{0:T(1024)(128)(4,1)}), s8[4194304]{0:T(1024)(128)(4,1)S(1)}, s32[]{:S(2)}) async-start(s8[5242880]{0:T(1024)(128)(4,1)} %bitcast.124), calls=%async_computation.1 | async-start | bytes 8388608
  189.8 4.5 %slice-start.2 = ((s8[5898240]{0:T(1024)(128)(4,1)}), s8[4194304]{0:T(1024)(128)(4,1)S(1)}, s32[]{:S(2)}) async-start(s8[5898240]{0:T(1024)(128)(4,1)} %bitcast.133), calls=%async_computation.3 | async-start | bytes 8388608
  191.0 4.4 %slice-start.1 = ((s8[5242880]{0:T(1024)(128)(4,1)}), s8[1048576]{0:T(1024)(128)(4,1)S(1)}, s32[]{:S(2)}) async-start(s8[5242880]{0:T(1024)(128)(4,1)} %bitcast.124), calls=%async_computation.2 | async-start | bytes 2097152
  212.3 11.7 %copy-start.9 = (f32[33,16,512]{2,1,0:T(8,128)S(1)}, f32[33,16,512]{2,1,0:T(8,128)}, u32[]{:S(2)}) copy-start(f32[33,16,512]{2,1,0:T(8,128)} %fusion.86) | copy-start | bytes 3244036
  212.3 11.7 %copy-start.10 = (f32[33,16,512]{2,1,0:T(8,128)S(1)}, f32[33,16,512]{2,1,0:T(8,128)}, u32[]{:S(2)}) copy-start(f32[33,16,512]{2,1,0:T(8,128)} %get-tuple-element.86) | copy-start | bytes 3244036
  212.3 11.7 %copy-start.11 = (f32[33,16,512]{2,1,0:T(8,128)S(1)}, f32[33,16,512]{2,1,0:T(8,128)}, u32[]{:S(2)}) copy-start(f32[33,16,512]{2,1,0:T(8,128)} %get-tuple-element.87) | copy-start | bytes 3244036
  212.3 11.7 %copy-start.14 = (f32[5,2,16,512]{3,2,1,0:T(8,128)S(1)}, f32[5,2,16,512]{3,2,1,0:T(8,128)}, u32[]{:S(2)}) copy-start(f32[5,2,16,512]{3,2,1,0:T(8,128)} %copy-done.12) | copy-start | bytes 983044
  224.0 6.4 %copy-start.15 = (f32[5,32,2,512]{3,2,1,0:T(2,128)S(1)}, f32[5,32,2,512]{3,2,1,0:T(2,128)}, u32[]{:S(2)}) copy-start(f32[5,32,2,512]{3,2,1,0:T(2,128)} %rev.8) | copy-start | bytes 1966084
  224.0 6.4 %copy-start.16 = (f32[5,32,2,512]{3,2,1,0:T(2,128)S(1)}, f32[5,32,2,512]{3,2,1,0:T(2,128)}, u32[]{:S(2)}) copy-start(f32[5,32,2,512]{3,2,1,0:T(2,128)} %rev.7) | copy-start | bytes 1966084
  224.0 6.4 %copy-start.20 = (f32[5]{0:T(128)S(1)}, f32[5]{0:T(128)}, u32[]{:S(2)}) copy-start(f32[5]{0:T(128)} %constant.282.clone) | copy-start | bytes 64
  242.6 8.3 %copy-start.17 = (f32[1,32,16,512]{3,2,1,0:T(8,128)S(1)}, f32[1,32,16,512]{3,2,1,0:T(8,128)}, u32[]{:S(2)}) copy-start(f32[1,32,16,512]{3,2,1,0:T(8,128)} %param.23) | copy-start | bytes 3145732
  242.6 8.3 %copy-start.18 = (f32[512,512,1,1]{1,0,3,2:T(8,128)S(1)}, f32[512,512,1,1]{1,0,3,2:T(8,128)}, u32[]{:S(2)}) copy-start(f32[512,512,1,1]{1,0,3,2:T(8,128)} %constant.359) | copy-start | bytes 3145732
  273.2 12.0 %collective-permute-start.6 = (f32[5,2,16,512]{3,2,1,0:T(8,128)S(1)}, f32[5,2,16,512]{3,2,1,0:T(8,128)S(1)}, u32[]{:S(2)}, u32[]{:S(2)}) collective-permute-start(f32[5,2,16,512]{3,2,1,0:T(8,128)S(1)} %get-tuple-element.97), channel_id=1, source_target_pairs={{4,0},{8,4},{12,8},{16,12},{20,16},{24,20},{28,24},{32,28},{36,32}... | collective-permute-start | bytes 983048 | tf_op jit(solution)/shard_map/ppermute | solution.py:72
  278.0 12.6 %collective-permute-start.5 = (f32[5,2,16,512]{3,2,1,0:T(8,128)S(1)}, f32[5,2,16,512]{3,2,1,0:T(8,128)S(1)}, u32[]{:S(2)}, u32[]{:S(2)}) collective-permute-start(f32[5,2,16,512]{3,2,1,0:T(8,128)S(1)} %get-tuple-element.96), channel_id=1, source_target_pairs={{0,4},{4,8},{8,12},{12,16},{16,20},{20,24},{24,28},{28,32},{32,36}... | collective-permute-start | bytes 983048 | tf_op jit(solution)/shard_map/ppermute | solution.py:69
  290.6 23.0 %copy-start.1 = (f32[5,32,16,512]{3,2,1,0:T(8,128)S(1)}, f32[5,32,16,512]{3,2,1,0:T(8,128)}, u32[]{:S(2)}) copy-start(f32[5,32,16,512]{3,2,1,0:T(8,128)} %fusion.46) | copy-start | bytes 15728644
  294.2 18.0 %collective-permute-start.8 = (f32[5,36,2,512]{3,2,1,0:T(2,128)S(1)}, f32[5,36,2,512]{3,2,1,0:T(2,128)S(1)}, u32[]{:S(2)}, u32[]{:S(2)}) collective-permute-start(f32[5,36,2,512]{3,2,1,0:T(2,128)S(1)} %get-tuple-element.95), channel_id=1, source_target_pairs={{1,0},{2,1},{3,2},{0,3},{5,4},{6,5},{7,6},{4,7},{9,8},{10,9},{11,1... | collective-permute-start | bytes 2211848 | tf_op jit(solution)/shard_map/ppermute | solution.py:72
  295.3 18.4 %collective-permute-start.7 = (f32[5,36,2,512]{3,2,1,0:T(2,128)S(1)}, f32[5,36,2,512]{3,2,1,0:T(2,128)S(1)}, u32[]{:S(2)}, u32[]{:S(2)}) collective-permute-start(f32[5,36,2,512]{3,2,1,0:T(2,128)S(1)} %get-tuple-element.94), channel_id=1, source_target_pairs={{0,1},{1,2},{2,3},{3,0},{4,5},{5,6},{6,7},{7,4},{8,9},{9,10},{10,1... | collective-permute-start | bytes 2211848 | tf_op jit(solution)/shard_map/ppermute | solution.py:69
  (12 other events, 27.8 us)
where the time goes:
time: 336 us; the launch traced here: 329 us
  local copies, waits for them, and re-layouts  158 us (47%)
  other arithmetic  96.5 us (29%)
  waiting for transfers between devices  28.5 us (8%)
  starting transfers between devices  23.7 us (7%)
  matrix products  21.2 us (6%)
    gather x5, local copies, waits for them, and re-layouts, on_device(): jnp.take_along_axis(plane_cycle, jnp.broadcast_to(trail_index[None, None]...  63.2 us
    gather x5, local copies, waits for them, and re-layouts, on_device(): jnp.take_along_axis(plane_cycle, jnp.broadcast_to(lead_index[None, None],...  61.9 us
    sub x3, other arithmetic, flux_balance(): 0.5 * (slab_cut(fluxes, 1, length + 1, direction) + slab_cut(fluxes, 2, l...  26.2 us
    ppermute x2, waiting for transfers between devices, padded(): lax.ppermute(lax.slice_in_dim(block, 0, width, axis=dim), axis, backward)  21.5 us
    dot_general x1, matrix products, on_device(): jnp.dot(increment_raw.reshape(-1, count_a), inverse, precision=lax.Precis...  21.2 us
    unnamed x54, local copies, waits for them, and re-layouts  7.72 us
    mul x4, other arithmetic, flux_balance(): fluxes = margin * relative  7.56 us
    ppermute x2, waiting for transfers between devices, padded(): lax.ppermute(lax.slice_in_dim(block, block.shape[dim] - width, None, axis...  6.94 us
  transfers between devices with their start and end apart: 10, of which 4 were waited for; matrix products, arithmetic and copies ran while one was open for 62% of the time, Pallas kernels for 0%

commit v1 on v0

v1 whole, which is shorter than its diff:
```python
import functools

import jax
import jax.numpy as jnp
import numpy as np
from jax import lax
from jax.experimental import pallas as pl
from jax.experimental.pallas import tpu as pltpu
from jax.sharding import PartitionSpec as P

GAMMA = 1.4
GAMMA_LESS = 0.4
SECOND_COEF = 0.5
FOURTH_COEF = 0.03125
RATE = 0.75
GRID_SPEED = 0.5
AXIAL_COUPLING = 0.8
CIRC_COUPLING = 0.6
RADIAL_COUPLING = 0.6

NCOMP = 5
LANES = 128
ROWS = 32
FIRST = 8
MIB = 1 << 20


def axial_table(length):
    modes_index = np.arange(1, length + 1) * 1.0
    angle = np.pi / (length + 1)
    modes = np.sin(np.outer(modes_index, modes_index) * angle)
    eigen = 1.0 + 2.0 * AXIAL_COUPLING - 2.0 * AXIAL_COUPLING * np.cos(modes_index * angle)
    return modes / eigen[None, :] @ modes.T * (2.0 / (length + 1))


def vmem():
    return pl.BlockSpec(memory_space=pltpu.VMEM)


def smem():
    return pl.BlockSpec(memory_space=pltpu.SMEM)


def hbm():
    return pl.BlockSpec(memory_space=pl.ANY)


def lane_index(rows):
    return lax.broadcasted_iota(jnp.int32, (rows, LANES), 1)


def edges_kernel(flags, state, rad_low, rad_high, circ_low, circ_high, face, buf, sems):
    planes = state.shape[1]
    chunks = state.shape[3] // LANES
    group = 8
    copies = []
    for g in range(planes // group):
        copy = pltpu.make_async_copy(
            state.at[:, pl.ds(g * group, group)], buf.at[:, pl.ds(g * group, group)], sems.at[g]
        )
        copy.start()
        copies.append(copy)
    rotor = flags[2]
    lane = lane_index(8)
    sub = lax.broadcasted_iota(jnp.int32, (8, LANES), 0)
    for g in range(planes // group):
        copies[g].wait()

        def body(j, carry):
            for m in range(NCOMP):
                for c in range(chunks):
                    cols = pl.ds(c * LANES, LANES)
                    rad_low[m, j, pl.ds(2 * c, 2), :] = buf[m, j, 0:2, cols]
                    rad_high[m, j, pl.ds(2 * c, 2), :] = buf[m, j, 14:16, cols]
            for h in range(2):
                total = jnp.zeros((8, LANES), jnp.float32)
                for m in range(NCOMP):
                    front = buf[m, j, 8 * h : 8 * h + 8, 0:LANES]
                    back = buf[m, j, 8 * h : 8 * h + 8, (chunks - 1) * LANES : chunks * LANES]
                    first = pltpu.roll(front, 2 * m, 1, stride=16, stride_axis=0)
                    last = pltpu.roll(back, 2 * m + 2, 1, stride=16, stride_axis=0)
                    moved = jnp.where(rotor == 1, first, last)
                    at = lane - sub * 16 - 2 * m
                    total = jnp.where((at >= 0) & (at < 2), moved, total)
                face[h, pl.ds(j, 1), :] = jnp.sum(total, axis=0, keepdims=True)
            return carry

        lax.fori_loop(g * group, (g + 1) * group, body, 0)
    circ_low[...] = buf[:, 0:2]
    circ_high[...] = buf[:, planes - 2 : planes]


def edges(flags, cells):
    planes, rows, length = cells.shape[1:]
    rad = jax.ShapeDtypeStruct((NCOMP, planes, 8, LANES), jnp.float32)
    circ = jax.ShapeDtypeStruct((NCOMP, 2, rows, length), jnp.float32)
    face = jax.ShapeDtypeStruct((2, planes, LANES), jnp.float32)
    return pl.pallas_call(
        edges_kernel,
        out_shape=(rad, rad, circ, circ, face),
        in_specs=[smem(), hbm()],
        out_specs=(vmem(),) * 5,
        scratch_shapes=[pltpu.VMEM(cells.shape, jnp.float32), pltpu.SemaphoreType.DMA((4,))],
        compiler_params=pltpu.CompilerParams(vmem_limit_bytes=24 * MIB),
        name="state_edges",
    )(flags, cells)


def primitives(cons):
    inverse = 1.0 / cons[0]
    velocity = [cons[m] * inverse for m in (1, 2, 3)]
    kinetic = cons[1] * velocity[0] + cons[2] * velocity[1] + cons[3] * velocity[2]
    pressure = GAMMA_LESS * (cons[4] - 0.5 * kinetic)
    square = GAMMA * pressure * inverse
    sound = square * lax.rsqrt(square)
    return [pressure, sound, *velocity]


def sensor_of(upper, middle, lower):
    outer = upper + lower
    twice = 2.0 * middle
    return jnp.abs(outer - twice) / (outer + twice)


def face_flux(component, cons, pressure, sound, velocity, sensor, grid_speed):
    half = [0.5 * (v - grid_speed) if grid_speed is not None else 0.5 * v for v in velocity]
    speed = jnp.abs(half[0]) + jnp.abs(half[1]) + 0.5 * (sound[0] + sound[1])
    second = SECOND_COEF * jnp.maximum(sensor[0], sensor[1])
    fourth = jnp.maximum(0.0, FOURTH_COEF - second)
    outer = speed * fourth
    inner = speed * (second + 3.0 * fourth)
    near = half[0] + inner
    far = half[1] - inner
    fluxes = []
    for m in range(NCOMP):
        before, left, right, beyond = cons[m]
        flux = right * far + left * near + outer * (beyond - before)
        if m == component:
            flux = flux + 0.5 * (pressure[0] + pressure[1])
        if m == 4:
            flux = flux + 0.5 * (pressure[0] * velocity[0] + pressure[1] * velocity[1])
        fluxes.append(flux)
    return fluxes


def flux_kernel(
    flags,
    starts,
    lead_weight,
    trail_weight,
    state,
    source,
    pseudo,
    circ_low,
    circ_high,
    rad_low,
    rad_high,
    plane,
    table_high,
    table_low,
    out,
    out_circ_low,
    out_circ_high,
    out_rad_low,
    out_rad_high,
    cons,
    prim,
    src,
    step,
    raw_high,
    raw_low,
    result,
    tables,
    halo_low,
    halo_high,
    cycle,
    ghosts,
    circ_flux,
    circ_sensor,
    rad_flux,
    sems,
):
    planes = state.shape[1]
    chunks = state.shape[3] // LANES
    group = 8
    groups = planes // group
    cells = pl.ds(FIRST, 16)

    def start(a, b, s):
        copy = pltpu.make_async_copy(a, b, s)
        copy.start()
        return copy

    loads = []
    for g in range(groups):
        part = [
            start(
                state.at[:, pl.ds(g * group, group), :, pl.ds(c * LANES, LANES)],
                cons.at[:, pl.ds(2 + g * group, group), c, cells, :],
                sems.at[g * chunks + c],
            )
            for c in range(chunks)
        ]
        loads.append(part)
    k = groups * chunks
    halos = []
    for c in range(chunks):
        cols = pl.ds(c * LANES, LANES)
        halos.append(start(circ_low.at[:, :, :, cols], cons.at[:, 0:2, c, cells, :], sems.at[k]))
        halos.append(
            start(
                circ_high.at[:, :, :, cols],
                cons.at[:, planes + 2 : planes + 4, c, cells, :],
                sems.at[k + 1],
            )
        )
        k += 2
    halos.append(start(rad_low, halo_low, sems.at[k]))
    halos.append(start(rad_high, halo_high, sems.at[k + 1]))
    k += 2
    late = [
        start(pseudo, step, sems.at[k]),
        start(source, src, sems.at[k + 1]),
        start(table_high, tables.at[0], sems.at[k + 2]),
        start(table_low, tables.at[1], sems.at[k + 3]),
    ]
    k += 4

    rotor = flags[2]
    lane8 = lane_index(8)
    lane = lane_index(16)

    count = plane.shape[0]
    width = plane.shape[2]
    for h in range(2):
        for s in range(count):
            cycle[h, pl.ds(s * width, width), :] = plane[s, h]
        cycle[h, pl.ds(count * width, width), :] = plane[0, h]
        cycle[h, pl.ds((count + 1) * width, 8), :] = plane[1, h, 0:8]
    for h in range(2):
        for jt in range(planes // 8):
            total = jnp.zeros((8, LANES), jnp.float32)
            for r in range(8):
                at = starts[8 * h + r] + 8 * jt
                value = (
                    lead_weight[8 * h + r] * cycle[h, pl.ds(at, 8), :]
                    + trail_weight[8 * h + r] * cycle[h, pl.ds(at + 1, 8), :]
                )
                to = (8 - r) % 8
                if to != r:
                    value = pltpu.roll(value, (to - r) % 8 * 16, 1)
                total = jnp.where(lane8 // 16 == to, value, total)
            ghosts[h, pl.ds(8 * jt, 8), :] = jnp.where(
                rotor == 1, pltpu.roll(total, LANES - 2, 1), total
            )

    for part in loads:
        for copy in part:
            copy.wait()
    for copy in halos:
        copy.wait()

    def mirror(edge, first):
        def body(j, carry):
            for m in range(NCOMP):
                for c in range(chunks):
                    a = cons[m, j + 2, c, pl.ds(first, 1), :]
                    b = cons[m, j + 2, c, pl.ds(first + 1, 1), :]
                    if m == 3:
                        a, b = -a, -b
                    edge[m, j, pl.ds(2 * c, 1), :] = b
                    edge[m, j, pl.ds(2 * c + 1, 1), :] = a
            return carry

        lax.fori_loop(0, planes, body, 0)

    @pl.when(flags[0] == 1)
    def _():
        mirror(halo_low, FIRST)

    @pl.when(flags[1] == 1)
    def _():
        mirror(halo_high, FIRST + 14)

    def prepare(j, carry):
        for c in range(chunks):
            fields = primitives([cons[m, j, c, cells, :] for m in range(NCOMP)])
            for f in range(NCOMP):
                prim[f, j, c, cells, :] = fields[f]
        return carry

    lax.fori_loop(0, planes + 4, prepare, 0)

    def prepare_halo(j, carry):
        for edge, row in ((halo_low, FIRST - 2), (halo_high, FIRST + 16)):
            packed = [edge[m, j] for m in range(NCOMP)]
            fields = primitives(packed)
            for c in range(chunks):
                for m in range(NCOMP):
                    cons[m, j + 2, c, pl.ds(row, 2), :] = edge[m, j, pl.ds(2 * c, 2), :]
                    prim[m, j + 2, c, pl.ds(row, 2), :] = fields[m][2 * c : 2 * c + 2]
        return carry

    lax.fori_loop(0, planes, prepare_halo, 0)
    for copy in late:
        copy.wait()

    spin = GRID_SPEED * rotor.astype(jnp.float32)

    def circ_face(j, c, sensor_before):
        p = [prim[0, j + d, c, cells, :] for d in (0, 1, 2)]
        sensor = sensor_of(p[2], p[1], p[0])
        flux = face_flux(
            2,
            [[cons[m, j + d, c, cells, :] for d in (-1, 0, 1, 2)] for m in range(NCOMP)],
            p[:2],
            [prim[1, j + d, c, cells, :] for d in (0, 1)],
            [prim[3, j + d, c, cells, :] for d in (0, 1)],
            [sensor_before, sensor],
            spin,
        )
        return flux, sensor

    for c in range(chunks):
        p = [prim[0, d, c, cells, :] for d in (0, 1, 2)]
        flux, sensor = circ_face(1, c, sensor_of(p[2], p[1], p[0]))
        circ_sensor[c] = sensor
        for m in range(NCOMP):
            circ_flux[m, c] = flux[m]

    ghost_lanes = jnp.where(lane < 64, 1 - rotor, rotor) == 1

    def behind(parts, by):
        turned = [pltpu.roll(x, by, 1) for x in parts]
        return [jnp.where(lane < by, turned[c - 1], turned[c]) for c in range(chunks + 1)]

    def ahead(parts):
        turned = [pltpu.roll(x, LANES - 1, 1) for x in parts]
        return [
            jnp.where(lane < LANES - 1, turned[c], turned[(c + 1) % (chunks + 1)])
            for c in range(chunks + 1)
        ]

    def plane_body(j, carry):
        at = j + 2
        spread = jnp.concatenate(
            [
                pltpu.roll(
                    jnp.broadcast_to(ghosts[h, pl.ds(j, 1), :], (8, LANES)),
                    0,
                    1,
                    stride=16,
                    stride_axis=0,
                )
                for h in range(2)
            ],
            axis=0,
        )
        axial = []
        for m in range(NCOMP):
            parts = [cons[m, at, c, cells, :] for c in range(chunks)]
            moved = pltpu.roll(spread, LANES - 2 * m, 1) if m else spread
            edge = jnp.where(
                rotor == 1,
                jnp.broadcast_to(parts[chunks - 1][:, LANES - 1 : LANES], (16, LANES)),
                jnp.broadcast_to(parts[0][:, 0:1], (16, LANES)),
            )
            parts.append(jnp.where(ghost_lanes, moved, edge))
            axial.append(parts)
        fields = [[prim[f, at, c, cells, :] for c in range(chunks)] for f in (0, 1, 2)]
        extra = primitives([axial[m][chunks] for m in range(NCOMP)])
        for f in range(3):
            fields[f].append(extra[f])
        p, sound, speed = fields
        p_before = behind(p, 1)
        p_after = ahead(p)
        sensor = [sensor_of(p_after[c], p[c], p_before[c]) for c in range(chunks + 1)]
        sensor_before = behind(sensor, 1)
        sound_before = behind(sound, 1)
        speed_before = behind(speed, 1)
        shifted = [(behind(x, 2), behind(x, 1), x, ahead(x)) for x in axial]
        axial_flux = [
            face_flux(
                1,
                [[shifted[m][d][c] for d in range(4)] for m in range(NCOMP)],
                [p_before[c], p[c]],
                [sound_before[c], sound[c]],
                [speed_before[c], speed[c]],
                [sensor_before[c], sensor[c]],
                None,
            )
            for c in range(chunks + 1)
        ]
        balance = []
        for m in range(NCOMP):
            parts = [axial_flux[c][m] for c in range(chunks + 1)]
            upper = ahead(parts)
            balance.append([upper[c] - parts[c] for c in range(chunks)])

        for c in range(chunks):
            flux, sensor_next = circ_face(at, c, circ_sensor[c])
            circ_sensor[c] = sensor_next
            def rows(ref, f, d):
                return ref[f, at, c, pl.ds(FIRST + d, 24 if d < 1 else 23), :]

            tall = pl.ds(FIRST - 0, 24)
            pressures = [prim[0, at, c, pl.ds(FIRST + d, 17), :] for d in (-2, -1, 0, 1)]
            radial = face_flux(
                3,
                [
                    [cons[m, at, c, pl.ds(FIRST + d, 17), :] for d in (-2, -1, 0, 1)]
                    for m in range(NCOMP)
                ],
                pressures[1:3],
                [prim[1, at, c, pl.ds(FIRST + d, 17), :] for d in (-1, 0)],
                [prim[4, at, c, pl.ds(FIRST + d, 17), :] for d in (-1, 0)],
                [
                    sensor_of(pressures[2], pressures[1], pressures[0]),
                    sensor_of(pressures[3], pressures[2], pressures[1]),
                ],
                None,
            )
            pace = step[j, :, pl.ds(c * LANES, LANES)]
            for m in range(NCOMP):
                rad_flux[m, c, 0:17, :] = radial[m]
                total = balance[m][c] + (flux[m] - circ_flux[m, c])
                circ_flux[m, c] = flux[m]
                total = total + (rad_flux[m, c, pl.ds(1, 16), :] - rad_flux[m, c, pl.ds(0, 16), :])
                raw = pace * (
                    total + RATE * cons[m, at, c, cells, :] + src[m, j, :, pl.ds(c * LANES, LANES)]
                )
                high = raw.astype(jnp.bfloat16)
                raw_high[m, j, :, pl.ds(c * LANES, LANES)] = high
                raw_low[m, j, :, pl.ds(c * LANES, LANES)] = (raw - high.astype(jnp.float32)).astype(
                    jnp.bfloat16
                )
        return carry

    lax.fori_loop(0, planes, plane_body, 0)

    def solve(q, carry):
        length = chunks * LANES
        for m in range(NCOMP):
            high = raw_high[m, pl.ds(q * 8, 8)].reshape(128, length)
            low = raw_low[m, pl.ds(q * 8, 8)].reshape(128, length)
            value = (
                jnp.dot(high, tables[0], preferred_element_type=jnp.float32)
                + jnp.dot(high, tables[1], preferred_element_type=jnp.float32)
                + jnp.dot(low, tables[0], preferred_element_type=jnp.float32)
            )
            result[m, pl.ds(q * 8, 8)] = value.reshape(8, 16, length)
        return carry

    lax.fori_loop(0, planes // 8, solve, 0)

    stores = [
        start(result, out, sems.at[k]),
        start(result.at[:, 0:2], out_circ_low, sems.at[k + 1]),
        start(result.at[:, planes - 2 : planes], out_circ_high, sems.at[k + 2]),
    ]

    def pick(j, carry):
        for m in range(NCOMP):
            for c in range(chunks):
                cols = pl.ds(c * LANES, LANES)
                out_rad_low[m, j, pl.ds(2 * c, 2), :] = result[m, j, 0:2, cols]
                out_rad_high[m, j, pl.ds(2 * c, 2), :] = result[m, j, 14:16, cols]
        return carry

    lax.fori_loop(0, planes, pick, 0)
    for copy in stores:
        copy.wait()


def fluxes(flags, starts, lead, trail, cells, source, pseudo, halos, plane):
    planes, rows, length = cells.shape[1:]
    chunks = length // LANES
    table = -axial_table(length).astype(np.float32)
    table_high = table.astype(jnp.bfloat16)
    table_low = (table - table_high.astype(np.float32)).astype(jnp.bfloat16)
    f32 = jnp.float32
    rad = jax.ShapeDtypeStruct((NCOMP, planes, 8, LANES), f32)
    circ = jax.ShapeDtypeStruct((NCOMP, 2, rows, length), f32)
    groups = planes // 8
    return pl.pallas_call(
        flux_kernel,
        out_shape=(jax.ShapeDtypeStruct(cells.shape, f32), circ, circ, rad, rad),
        in_specs=[smem()] * 4 + [hbm()] * 7 + [vmem()] + [hbm()] * 2,
        out_specs=(hbm(),) * 3 + (vmem(),) * 2,
        scratch_shapes=[
            pltpu.VMEM((NCOMP, planes + 4, chunks, ROWS, LANES), f32),
            pltpu.VMEM((NCOMP, planes + 4, chunks, ROWS, LANES), f32),
            pltpu.VMEM(cells.shape, f32),
            pltpu.VMEM(pseudo.shape, f32),
            pltpu.VMEM(cells.shape, jnp.bfloat16),
            pltpu.VMEM(cells.shape, jnp.bfloat16),
            pltpu.VMEM(cells.shape, f32),
            pltpu.VMEM((2, length, length), jnp.bfloat16),
            pltpu.VMEM((NCOMP, planes, 8, LANES), f32),
            pltpu.VMEM((NCOMP, planes, 8, LANES), f32),
            pltpu.VMEM((2, plane.shape[0] * planes + planes + 8, LANES), f32),
            pltpu.VMEM((2, planes, LANES), f32),
            pltpu.VMEM((NCOMP, chunks, rows, LANES), f32),
            pltpu.VMEM((chunks, rows, LANES), f32),
            pltpu.VMEM((NCOMP, chunks, 24, LANES), f32),
            pltpu.SemaphoreType.DMA((groups * chunks + 2 * chunks + 9,)),
        ],
        compiler_params=pltpu.CompilerParams(vmem_limit_bytes=58 * MIB),
        name="row_fluxes",
    )(
        flags,
        starts,
        lead,
        trail,
        cells,
        source,
        pseudo,
        *halos,
        plane,
        jnp.asarray(table_high),
        jnp.asarray(table_low),
    )


def smooth_kernel(flags, field, circ_low, circ_high, rad_low, rad_high, ll, lh, hl, hh, out, buf, mid, done, sems):
    planes = field.shape[1]
    chunks = field.shape[3] // LANES
    cells = pl.ds(FIRST, 16)
    group = 8

    def start(a, b, s):
        copy = pltpu.make_async_copy(a, b, s)
        copy.start()
        return copy

    copies = []
    k = 0
    for c in range(chunks):
        cols = pl.ds(c * LANES, LANES)
        copies.append(start(field.at[:, :, :, cols], buf.at[:, 2 : planes + 2, c, cells, :], sems.at[k]))
        copies.append(start(circ_low.at[:, :, :, cols], buf.at[:, 0:2, c, cells, :], sems.at[k + 1]))
        copies.append(
            start(circ_high.at[:, :, :, cols], buf.at[:, planes + 2 : planes + 4, c, cells, :], sems.at[k + 2])
        )
        k += 3

    def put(low, high, first, count):
        def body(j, carry):
            for m in range(NCOMP):
                for c in range(chunks):
                    buf[m, first + j, c, pl.ds(FIRST - 2, 2), :] = low[m, j, pl.ds(2 * c, 2), :]
                    buf[m, first + j, c, pl.ds(FIRST + 16, 2), :] = high[m, j, pl.ds(2 * c, 2), :]
            return carry

        lax.fori_loop(0, count, body, 0)

    put(rad_low, rad_high, 2, planes)
    put(ll, lh, 0, 2)
    put(hl, hh, planes + 2, 2)
    for copy in copies:
        copy.wait()

    def wall(zero_row, odd_row, from_row):
        def body(j, carry):
            for m in range(NCOMP):
                for c in range(chunks):
                    buf[m, j, c, pl.ds(zero_row, 1), :] = jnp.zeros((1, LANES), jnp.float32)
                    buf[m, j, c, pl.ds(odd_row, 1), :] = -buf[m, j, c, pl.ds(from_row, 1), :]
            return carry

        lax.fori_loop(0, planes + 4, body, 0)

    @pl.when(flags[0] == 1)
    def _():
        wall(FIRST - 1, FIRST - 2, FIRST)

    @pl.when(flags[1] == 1)
    def _():
        wall(FIRST + 16, FIRST + 17, FIRST + 15)

    def weights(coupling):
        own = 1.0 / (1.0 + 2.0 * coupling)
        side = coupling / (1.0 + 2.0 * coupling)
        return own * own + 2.0 * side * side, 2.0 * own * side, side * side

    def radial(j, carry):
        w0, w1, w2 = weights(RADIAL_COUPLING)
        for m in range(NCOMP):
            for c in range(chunks):
                x = [buf[m, j, c, pl.ds(FIRST + d, 16), :] for d in (-2, -1, 0, 1, 2)]
                mid[m, j, c] = w0 * x[2] + w1 * (x[1] + x[3]) + w2 * (x[0] + x[4])
        return carry

    lax.fori_loop(0, planes + 4, radial, 0)

    def around(j, carry):
        w0, w1, w2 = weights(CIRC_COUPLING)
        for m in range(NCOMP):
            for c in range(chunks):
                x = [mid[m, j + d, c] for d in range(5)]
                done[m, j, :, pl.ds(c * LANES, LANES)] = (
                    w0 * x[2] + w1 * (x[1] + x[3]) + w2 * (x[0] + x[4])
                )
        return carry

    stores = []
    for g in range(planes // group):
        lax.fori_loop(g * group, (g + 1) * group, around, 0)
        stores.append(
            start(done.at[:, pl.ds(g * group, group)], out.at[:, pl.ds(g * group, group)], sems.at[k])
        )
        k += 1
    for copy in stores:
        copy.wait()


def smoothed(flags, field, halos):
    planes, rows, length = field.shape[1:]
    chunks = length // LANES
    f32 = jnp.float32
    return pl.pallas_call(
        smooth_kernel,
        out_shape=jax.ShapeDtypeStruct(field.shape, f32),
        in_specs=[smem()] + [hbm()] * 3 + [vmem()] * 6,
        out_specs=hbm(),
        scratch_shapes=[
            pltpu.VMEM((NCOMP, planes + 4, chunks, ROWS, LANES), f32),
            pltpu.VMEM((NCOMP, planes + 4, chunks, rows, LANES), f32),
            pltpu.VMEM(field.shape, f32),
            pltpu.SemaphoreType.DMA((3 * chunks + planes // 8,)),
        ],
        compiler_params=pltpu.CompilerParams(vmem_limit_bytes=50 * MIB),
        name="smoothing",
    )(flags, field, *halos)


def ring(count):
    return [(i, (i + 1) % count) for i in range(count)]


def line(count):
    return [(i, i + 1) for i in range(count - 1)]


def back(pairs):
    return [(b, a) for a, b in pairs]


def diagonal(circ_pairs, rad_pairs, rads):
    return [(a * rads + c, b * rads + d) for a, b in circ_pairs for c, d in rad_pairs]


def on_device(state, time_source, pseudo_step, offsets, weights):
    cells = state[0]
    source = time_source[0]
    pseudo = pseudo_step[0]
    planes = cells.shape[1]
    circs = lax.axis_size("circ")
    rads = lax.axis_size("rad")
    total = planes * circs
    row = lax.axis_index("row")
    rad = lax.axis_index("rad")
    rotor = row == 1
    flags = jnp.stack(
        [(rad == 0).astype(jnp.int32), (rad == rads - 1).astype(jnp.int32), row.astype(jnp.int32)]
    )
    up_circ, up_rad = ring(circs), line(rads)

    rad_low, rad_high, circ_low, circ_high, face = edges(flags, cells)
    facing = lax.ppermute(face, "row", [(0, 1), (1, 0)])
    halo_circ_low = lax.ppermute(circ_high, "circ", up_circ)
    halo_circ_high = lax.ppermute(circ_low, "circ", back(up_circ))
    halo_rad_low = lax.ppermute(rad_high, "rad", up_rad)
    halo_rad_high = lax.ppermute(rad_low, "rad", back(up_rad))
    plane = lax.all_to_all(
        jnp.broadcast_to(facing[None], (circs, *facing.shape)), "circ", 0, 0, tiled=True
    )

    here = lax.axis_index("circ") * planes
    shift = offsets.astype(jnp.int32)
    starts = jnp.where(rotor, here + shift, here - shift - 1) % total
    lead = jnp.where(rotor, 1.0 - weights, weights)
    trail = jnp.where(rotor, weights, 1.0 - weights)

    field, circ_low, circ_high, rad_low, rad_high = fluxes(
        flags,
        starts,
        lead,
        trail,
        cells,
        source,
        pseudo,
        (halo_circ_low, halo_circ_high, halo_rad_low, halo_rad_high),
        plane,
    )
    both = ("circ", "rad")
    halos = (
        lax.ppermute(circ_high, "circ", up_circ),
        lax.ppermute(circ_low, "circ", back(up_circ)),
        lax.ppermute(rad_high, "rad", up_rad),
        lax.ppermute(rad_low, "rad", back(up_rad)),
        lax.ppermute(rad_high[:, planes - 2 :], both, diagonal(up_circ, up_rad, rads)),
        lax.ppermute(rad_low[:, planes - 2 :], both, diagonal(up_circ, back(up_rad), rads)),
        lax.ppermute(rad_high[:, :2], both, diagonal(back(up_circ), up_rad, rads)),
        lax.ppermute(rad_low[:, :2], both, diagonal(back(up_circ), back(up_rad), rads)),
    )
    return smoothed(flags, field, halos)[None]


def solution(mesh):
    return jax.shard_map(
        on_device,
        mesh=mesh,
        in_specs=(
            P("row", None, "circ", "rad", None),
            P("row", None, "circ", "rad", None),
            P("row", "circ", "rad", None),
            P("rad"),
            P("rad"),
        ),
        out_specs=P("row", None, "circ", "rad", None),
        check_vma=False,
    )
```

time: 336 us -> 145 us (0.43); the launches traced: 329 us -> 144 us
  local copies, waits for them, and re-layouts: 158 us -> 6.69 us
  other arithmetic: 96.5 us -> 1.2 us
  Pallas kernels: 0 us -> 52.1 us
  starting transfers between devices: 23.7 us -> 49.1 us
  matrix products: 21.2 us -> 0 us
  waiting for transfers between devices: 28.5 us -> 34.7 us
    gather x10 -> x0, local copies, waits for them, and re-layouts: 125 us -> none  [the longest x5 63.2 us: on_device(): jnp.take_along_axis(plane_cycle, jnp.broadcast_to(trail_index[None, None]...]
    pallas_call x0 -> x3, Pallas kernels: none -> 52.1 us  [the longest x1 39.4 us: fluxes(): pl.pallas_call(flux_kernel, out_shape=(jax.ShapeDtypeStruct(cells.shape,...]
    sub x3 -> x0, other arithmetic: 26.2 us -> none  [flux_balance(): 0.5 * (slab_cut(fluxes, 1, length + 1, direction) + slab_cut(fluxes, 2, l...]
    dot_general x1 -> x0, matrix products: 21.2 us -> none  [on_device(): jnp.dot(increment_raw.reshape(-1, count_a), inverse, precision=lax.Precis...]
    ppermute x9 -> x13, starting transfers between devices: 20 us -> 41.1 us  [the longest x1 8.35 us: on_device(): lax.ppermute(rad_high, 'rad', up_rad)]
    concatenate x4 -> x0, other arithmetic: 12.7 us -> none  [the longest x1 4.58 us: on_device(): axial_margin = jnp.concatenate([left_rim, cells, right_rim], axis=3)]
    select_n x6 -> x2, other arithmetic: 13 us -> 1.13 us  [the longest x1 0.59 us: on_device(): trail = jnp.where(rotor, weights, 1.0 - weights)]
    mul x10 -> x0, other arithmetic: 10.5 us -> none  [the longest x4 7.56 us: flux_balance(): fluxes = margin * relative]
  transfers between devices with their start and end apart: 10 -> 14, of which waited for: 4 -> 5; matrix products, arithmetic and copies ran while one was open for 62% -> 3% of each run, Pallas kernels for 0% -> 0%
where the time goes in v1:
time: 145 us; the launch traced here: 144 us
  Pallas kernels  52.1 us (36%)
  starting transfers between devices  49.1 us (34%)
  waiting for transfers between devices  34.7 us (24%)
  local copies, waits for them, and re-layouts  6.69 us (5%)
    pallas_call x1, Pallas kernels, fluxes(): pl.pallas_call(flux_kernel, out_shape=(jax.ShapeDtypeStruct(cells.shape,...  39.4 us
    ppermute x1, waiting for transfers between devices, on_device(): lax.ppermute(rad_low[:, planes - 2:], both, diagonal(up_circ, back(up_rad...  9.12 us
    ppermute x1, starting transfers between devices, on_device(): lax.ppermute(rad_high, 'rad', up_rad)  8.35 us
    pallas_call x1, Pallas kernels, smoothed(): pl.pallas_call(smooth_kernel, out_shape=jax.ShapeDtypeStruct(field.shape,...  8.32 us
    all_to_all x1, starting transfers between devices, on_device(): lax.all_to_all(jnp.broadcast_to(facing[None], (circs, *facing.shape)), 'c...  8.04 us
    ppermute x1, waiting for transfers between devices, on_device(): halo_circ_low = lax.ppermute(circ_high, 'circ', up_circ)  7.46 us
    ppermute x1, starting transfers between devices, on_device(): lax.ppermute(rad_high[:, :2], both, diagonal(back(up_circ), up_rad, rads))  7.07 us
    ppermute x1, waiting for transfers between devices, on_device(): facing = lax.ppermute(face, 'row', [(0, 1), (1, 0)])  6.37 us
  transfers between devices with their start and end apart: 14, of which 5 were waited for; matrix products, arithmetic and copies ran while one was open for 3% of the time, Pallas kernels for 0%

profile of v1, /device:TPU:1, one launch (start us, length us, event | category | flops | bytes accessed | tf_op | source)
XLA Modules:
  0.0 144.0 jit_solution(12058936968461916302)
XLA Ops:
  0.1 2.5 %copy-done = f32[1,5,32,16,512]{4,3,2,1,0:T(8,128)S(1)} copy-done((f32[1,5,32,16,512]{4,3,2,1,0:T(8,128)S(1)}, f32[1,5,32,16,512]{4,3,2,1,0:T(8,128)}, u32[]{:S(2)}) %copy-start) | copy-done | bytes 5242904
  2.6 4.4 %state_edges.1 = (f32[5,32,8,128]{3,2,1,0:T(8,128)S(1)}, f32[5,32,8,128]{3,2,1,0:T(8,128)S(1)}, f32[5,2,16,512]{3,2,1,0:T(8,128)S(1)}, f32[5,2,16,512]{3,2,1,0:T(8,128)S(1)}, f32[2,32,128]{2,1,0:T(8,128)S(1)}) custom-call(s32[3]{0:T(128)S(1)} %pad_add_fusion.flags, f32[5,32,16,512]{3,2,1,0:T(8,128)S(1)} %bitcast.8), custom_call_target="tpu_custom_call" | custom-call | tf_op jit(solution)/shard_map/state_edges/pallas_call | solution.py:98
  6.9 6.0 %collective-permute-start.2 = (f32[5,32,8,128]{3,2,1,0:T(8,128)S(1)}, f32[5,32,8,128]{3,2,1,0:T(8,128)S(1)}, u32[]{:S(2)}, u32[]{:S(2)}) collective-permute-start(f32[5,32,8,128]{3,2,1,0:T(8,128)S(1)} %get-tuple-element.17), channel_id=1, source_target_pairs={{0,1},{1,2},{2,3},{4,5},{5,6},{6,7},{8,9},{9,10},{10,11},{12,13},{... | collective-permute-start | bytes 1966088 | tf_op jit(solution)/shard_map/ppermute | solution.py:673
  13.0 1.9 %collective-permute-start.3 = (f32[5,32,8,128]{3,2,1,0:T(8,128)S(1)}, f32[5,32,8,128]{3,2,1,0:T(8,128)}, u32[]{:S(2)}, u32[]{:S(2)}) collective-permute-start(f32[5,32,8,128]{3,2,1,0:T(8,128)S(1)} %get-tuple-element.18), channel_id=1, source_target_pairs={{1,0},{2,1},{3,2},{5,4},{6,5},{7,6},{9,8},{10,9},{11,10},{13,12},{... | collective-permute-start | bytes 1966088 | tf_op jit(solution)/shard_map/ppermute | solution.py:674
  15.3 6.4 %collective-permute-done.4 = f32[2,32,128]{2,1,0:T(8,128)S(1)} collective-permute-done((f32[2,32,128]{2,1,0:T(8,128)S(1)}, f32[2,32,128]{2,1,0:T(8,128)S(1)}, u32[]{:S(2)}, u32[]{:S(2)}) %collective-permute-start.4) | collective-permute-done | bytes 32800 | tf_op jit(solution)/shard_map/ppermute | solution.py:670
  21.7 0.9 broadcast_in_dim.4
  22.5 8.0 %all-to-all-start = ((f32[16,2,32,128]{3,2,1,0:T(8,128)}), f32[16,2,32,128]{3,2,1,0:T(8,128)S(1)}, u32[]{:S(2)}, u32[]{:S(2)}) async-start(f32[16,2,32,128]{3,2,1,0:T(8,128)} %broadcast_in_dim.4), calls=%async_computation | async-start | bytes 1048576 | tf_op jit(solution)/shard_map/all_to_all | solution.py:675
  30.6 1.4 collective-permute-start
  31.9 3.5 %collective-permute-start.1 = (f32[5,2,16,512]{3,2,1,0:T(8,128)S(1)}, f32[5,2,16,512]{3,2,1,0:T(8,128)}, u32[]{:S(2)}, u32[]{:S(2)}) collective-permute-start(f32[5,2,16,512]{3,2,1,0:T(8,128)S(1)} %get-tuple-element.16), channel_id=1, source_target_pairs={{4,0},{8,4},{12,8},{16,12},{20,16},{24,20},{28,24},{32,28},{36,32}... | collective-permute-start | bytes 983048 | tf_op jit(solution)/shard_map/ppermute | solution.py:672
  36.6 7.5 %collective-permute-done.circ_low = f32[5,2,16,512]{3,2,1,0:T(8,128)S(1)} collective-permute-done((f32[5,2,16,512]{3,2,1,0:T(8,128)S(1)}, f32[5,2,16,512]{3,2,1,0:T(8,128)S(1)}, u32[]{:S(2)}, u32[]{:S(2)}) %collective-permute-start) | collective-permute-done | bytes 327712 | tf_op jit(solution)/shard_map/ppermute | solution.py:671
  45.1 39.4 %row_fluxes.1 = (f32[5,32,16,512]{3,2,1,0:T(8,128)}, f32[5,2,16,512]{3,2,1,0:T(8,128)}, f32[5,2,16,512]{3,2,1,0:T(8,128)}, f32[5,32,8,128]{3,2,1,0:T(8,128)}, f32[5,32,8,128]{3,2,1,0:T(8,128)}) custom-call(s32[3]{0:T(128)} %copy-done.1, s32[16]{0:T(128)} %and_select_fusion.starts, f32[16]{0:T(128)} %get-tuple-element.30.lead_weight, ...), custom_call_target="tpu_custom_call" | custom-call | tf_op jit(solution)/shard_map/row_fluxes/pallas_call | solution.py:485
  84.6 8.3 %collective-permute-start.7 = (f32[5,32,8,128]{3,2,1,0:T(8,128)}, f32[5,32,8,128]{3,2,1,0:T(8,128)S(1)}, u32[]{:S(2)}, u32[]{:S(2)}) collective-permute-start(f32[5,32,8,128]{3,2,1,0:T(8,128)} %get-tuple-element.23), channel_id=1, source_target_pairs={{0,1},{1,2},{2,3},{4,5},{5,6},{6,7},{8,9},{9,10},{10,11},{12,13},{... | collective-permute-start | bytes 1966088 | tf_op jit(solution)/shard_map/ppermute | solution.py:700
  92.9 1.9 %collective-permute-start.8 = (f32[5,32,8,128]{3,2,1,0:T(8,128)}, f32[5,32,8,128]{3,2,1,0:T(8,128)S(1)}, u32[]{:S(2)}, u32[]{:S(2)}) collective-permute-start(f32[5,32,8,128]{3,2,1,0:T(8,128)} %get-tuple-element.24), channel_id=1, source_target_pairs={{1,0},{2,1},{3,2},{5,4},{6,5},{7,6},{9,8},{10,9},{11,10},{13,12},{... | collective-permute-start | bytes 1966088 | tf_op jit(solution)/shard_map/ppermute | solution.py:701
  94.8 0.8 fusion.2
  95.7 7.1 %collective-permute-start.11 = (f32[5,2,8,128]{3,2,1,0:T(8,128)S(1)}, f32[5,2,8,128]{3,2,1,0:T(8,128)S(1)}, u32[]{:S(2)}, u32[]{:S(2)}) collective-permute-start(f32[5,2,8,128]{3,2,1,0:T(8,128)S(1)} %get-tuple-element.27), channel_id=1, source_target_pairs={{4,1},{5,2},{6,3},{8,5},{9,6},{10,7},{12,9},{13,10},{14,11},{16,13... | collective-permute-start | bytes 122888 | tf_op jit(solution)/shard_map/ppermute | solution.py:704
  102.8 4.8 %collective-permute-start.6 = (f32[5,2,16,512]{3,2,1,0:T(8,128)}, f32[5,2,16,512]{3,2,1,0:T(8,128)S(1)}, u32[]{:S(2)}, u32[]{:S(2)}) collective-permute-start(f32[5,2,16,512]{3,2,1,0:T(8,128)} %get-tuple-element.22), channel_id=1, source_target_pairs={{4,0},{8,4},{12,8},{16,12},{20,16},{24,20},{28,24},{32,28},{36,32}... | collective-permute-start | bytes 983048 | tf_op jit(solution)/shard_map/ppermute | solution.py:699
  107.6 1.9 %collective-permute-start.9 = (f32[5,2,8,128]{3,2,1,0:T(8,128)S(1)}, f32[5,2,8,128]{3,2,1,0:T(8,128)S(1)}, u32[]{:S(2)}, u32[]{:S(2)}) collective-permute-start(f32[5,2,8,128]{3,2,1,0:T(8,128)S(1)} %get-tuple-element.28), channel_id=1, source_target_pairs={{0,5},{1,6},{2,7},{4,9},{5,10},{6,11},{8,13},{9,14},{10,15},{12,17... | collective-permute-start | bytes 122888 | tf_op jit(solution)/shard_map/ppermute | solution.py:702
  109.5 0.8 fusion.1
  110.3 5.9 %collective-permute-done.9.ll = f32[5,2,8,128]{3,2,1,0:T(8,128)S(1)} collective-permute-done((f32[5,2,8,128]{3,2,1,0:T(8,128)S(1)}, f32[5,2,8,128]{3,2,1,0:T(8,128)S(1)}, u32[]{:S(2)}, u32[]{:S(2)}) %collective-permute-start.9) | collective-permute-done | bytes 40992 | tf_op jit(solution)/shard_map/ppermute | solution.py:702
  116.2 1.9 %collective-permute-start.12 = (f32[5,2,8,128]{3,2,1,0:T(8,128)S(1)}, f32[5,2,8,128]{3,2,1,0:T(8,128)S(1)}, u32[]{:S(2)}, u32[]{:S(2)}) collective-permute-start(f32[5,2,8,128]{3,2,1,0:T(8,128)S(1)} %get-tuple-element.25), channel_id=1, source_target_pairs={{5,0},{6,1},{7,2},{9,4},{10,5},{11,6},{13,8},{14,9},{15,10},{17,12... | collective-permute-start | bytes 122888 | tf_op jit(solution)/shard_map/ppermute | solution.py:705
  118.1 5.8 %collective-permute-done.12.hh = f32[5,2,8,128]{3,2,1,0:T(8,128)S(1)} collective-permute-done((f32[5,2,8,128]{3,2,1,0:T(8,128)S(1)}, f32[5,2,8,128]{3,2,1,0:T(8,128)S(1)}, u32[]{:S(2)}, u32[]{:S(2)}) %collective-permute-start.12) | collective-permute-done | bytes 40992 | tf_op jit(solution)/shard_map/ppermute | solution.py:705
  123.9 1.9 %collective-permute-start.10 = (f32[5,2,8,128]{3,2,1,0:T(8,128)S(1)}, f32[5,2,8,128]{3,2,1,0:T(8,128)S(1)}, u32[]{:S(2)}, u32[]{:S(2)}) collective-permute-start(f32[5,2,8,128]{3,2,1,0:T(8,128)S(1)} %get-tuple-element.26), channel_id=1, source_target_pairs={{1,4},{2,5},{3,6},{5,8},{6,9},{7,10},{9,12},{10,13},{11,14},{13,16... | collective-permute-start | bytes 122888 | tf_op jit(solution)/shard_map/ppermute | solution.py:703
  125.8 9.1 %collective-permute-done.10.lh = f32[5,2,8,128]{3,2,1,0:T(8,128)S(1)} collective-permute-done((f32[5,2,8,128]{3,2,1,0:T(8,128)S(1)}, f32[5,2,8,128]{3,2,1,0:T(8,128)S(1)}, u32[]{:S(2)}, u32[]{:S(2)}) %collective-permute-start.10) | collective-permute-done | bytes 40992 | tf_op jit(solution)/shard_map/ppermute | solution.py:703
  135.6 8.3 %smoothing.1 = f32[5,32,16,512]{3,2,1,0:T(8,128)} custom-call(s32[3]{0:T(128)S(1)} %copy-done.2, f32[5,32,16,512]{3,2,1,0:T(8,128)} %get-tuple-element.20.field, f32[5,2,16,512]{3,2,1,0:T(8,128)S(1)} %collective-permute-done.5.circ_low, f32[5,2,16,512]{3,2,1,0:T(8,128)S(1)} %collective-permute-done.6.circ_high, ...), custom_call_target="tpu_custom_call" | custom-call | tf_op jit(solution)/shard_map/smoothing/pallas_call | solution.py:621
  (29 shorter events, 3.4 us)
Async XLA Ops:
  0.0 35.4 %copy-start.6 = (s32[16]{0:T(128)S(1)}, s32[16]{0:T(128)}, u32[]{:S(2)}) copy-start(s32[16]{0:T(128)} %param.10) | copy-start | bytes 196
  0.0 36.0 %copy-start.7 = (f32[16]{0:T(128)S(1)}, f32[16]{0:T(128)}, u32[]{:S(2)}) copy-start(f32[16]{0:T(128)} %param.11) | copy-start | bytes 196
  0.1 44.0 %copy-start.1 = (s32[3]{0:T(128)}, s32[3]{0:T(128)S(1)}, u32[]{:S(2)}) copy-start(s32[3]{0:T(128)S(1)} %pad_add_fusion.flags) | copy-start | bytes 40
  0.1 2.5 %copy-start = (f32[1,5,32,16,512]{4,3,2,1,0:T(8,128)S(1)}, f32[1,5,32,16,512]{4,3,2,1,0:T(8,128)}, u32[]{:S(2)}) copy-start(f32[1,5,32,16,512]{4,3,2,1,0:T(8,128)} %param.7) | copy-start | bytes 15728644
  6.9 37.1 %collective-permute-start.2 = (f32[5,32,8,128]{3,2,1,0:T(8,128)S(1)}, f32[5,32,8,128]{3,2,1,0:T(8,128)S(1)}, u32[]{:S(2)}, u32[]{:S(2)}) collective-permute-start(f32[5,32,8,128]{3,2,1,0:T(8,128)S(1)} %get-tuple-element.17), channel_id=1, source_target_pairs={{0,1},{1,2},{2,3},{4,5},{5,6},{6,7},{8,9},{9,10},{10,11},{12,13},{... | collective-permute-start | bytes 1966088 | tf_op jit(solution)/shard_map/ppermute | solution.py:673
  13.0 31.1 %collective-permute-start.3 = (f32[5,32,8,128]{3,2,1,0:T(8,128)S(1)}, f32[5,32,8,128]{3,2,1,0:T(8,128)}, u32[]{:S(2)}, u32[]{:S(2)}) collective-permute-start(f32[5,32,8,128]{3,2,1,0:T(8,128)S(1)} %get-tuple-element.18), channel_id=1, source_target_pairs={{1,0},{2,1},{3,2},{5,4},{6,5},{7,6},{9,8},{10,9},{11,10},{13,12},{... | collective-permute-start | bytes 1966088 | tf_op jit(solution)/shard_map/ppermute | solution.py:674
  14.9 6.8 %collective-permute-start.4 = (f32[2,32,128]{2,1,0:T(8,128)S(1)}, f32[2,32,128]{2,1,0:T(8,128)S(1)}, u32[]{:S(2)}, u32[]{:S(2)}) collective-permute-start(f32[2,32,128]{2,1,0:T(8,128)S(1)} %get-tuple-element.19), channel_id=1, source_target_pairs={{0,64},{64,0},{1,65},{65,1},{2,66},{66,2},{3,67},{67,3},{4,68},{68... | collective-permute-start | bytes 98312 | tf_op jit(solution)/shard_map/ppermute | solution.py:670
  22.5 21.5 %all-to-all-start = ((f32[16,2,32,128]{3,2,1,0:T(8,128)}), f32[16,2,32,128]{3,2,1,0:T(8,128)S(1)}, u32[]{:S(2)}, u32[]{:S(2)}) async-start(f32[16,2,32,128]{3,2,1,0:T(8,128)} %broadcast_in_dim.4), calls=%async_computation | async-start | bytes 1048576 | tf_op jit(solution)/shard_map/all_to_all | solution.py:675
  30.6 13.4 %collective-permute-start = (f32[5,2,16,512]{3,2,1,0:T(8,128)S(1)}, f32[5,2,16,512]{3,2,1,0:T(8,128)S(1)}, u32[]{:S(2)}, u32[]{:S(2)}) collective-permute-start(f32[5,2,16,512]{3,2,1,0:T(8,128)S(1)} %get-tuple-element.15), channel_id=1, source_target_pairs={{0,4},{4,8},{8,12},{12,16},{16,20},{20,24},{24,28},{28,32},{32,36}... | collective-permute-start | bytes 983048 | tf_op jit(solution)/shard_map/ppermute | solution.py:671
  31.9 12.1 %collective-permute-start.1 = (f32[5,2,16,512]{3,2,1,0:T(8,128)S(1)}, f32[5,2,16,512]{3,2,1,0:T(8,128)}, u32[]{:S(2)}, u32[]{:S(2)}) collective-permute-start(f32[5,2,16,512]{3,2,1,0:T(8,128)S(1)} %get-tuple-element.16), channel_id=1, source_target_pairs={{4,0},{8,4},{12,8},{16,12},{20,16},{24,20},{28,24},{32,28},{36,32}... | collective-permute-start | bytes 983048 | tf_op jit(solution)/shard_map/ppermute | solution.py:672
  44.0 0.8 copy-start.5
  44.0 1.0 copy-start.3
  44.0 1.1 copy-start.4
  84.6 50.4 %collective-permute-start.7 = (f32[5,32,8,128]{3,2,1,0:T(8,128)}, f32[5,32,8,128]{3,2,1,0:T(8,128)S(1)}, u32[]{:S(2)}, u32[]{:S(2)}) collective-permute-start(f32[5,32,8,128]{3,2,1,0:T(8,128)} %get-tuple-element.23), channel_id=1, source_target_pairs={{0,1},{1,2},{2,3},{4,5},{5,6},{6,7},{8,9},{9,10},{10,11},{12,13},{... | collective-permute-start | bytes 1966088 | tf_op jit(solution)/shard_map/ppermute | solution.py:700
  92.9 42.1 %collective-permute-start.8 = (f32[5,32,8,128]{3,2,1,0:T(8,128)}, f32[5,32,8,128]{3,2,1,0:T(8,128)S(1)}, u32[]{:S(2)}, u32[]{:S(2)}) collective-permute-start(f32[5,32,8,128]{3,2,1,0:T(8,128)} %get-tuple-element.24), channel_id=1, source_target_pairs={{1,0},{2,1},{3,2},{5,4},{6,5},{7,6},{9,8},{10,9},{11,10},{13,12},{... | collective-permute-start | bytes 1966088 | tf_op jit(solution)/shard_map/ppermute | solution.py:701
  95.7 11.9 %collective-permute-start.11 = (f32[5,2,8,128]{3,2,1,0:T(8,128)S(1)}, f32[5,2,8,128]{3,2,1,0:T(8,128)S(1)}, u32[]{:S(2)}, u32[]{:S(2)}) collective-permute-start(f32[5,2,8,128]{3,2,1,0:T(8,128)S(1)} %get-tuple-element.27), channel_id=1, source_target_pairs={{4,1},{5,2},{6,3},{8,5},{9,6},{10,7},{12,9},{13,10},{14,11},{16,13... | collective-permute-start | bytes 122888 | tf_op jit(solution)/shard_map/ppermute | solution.py:704
  102.7 32.2 %collective-permute-start.5 = (f32[5,2,16,512]{3,2,1,0:T(8,128)}, f32[5,2,16,512]{3,2,1,0:T(8,128)S(1)}, u32[]{:S(2)}, u32[]{:S(2)}) collective-permute-start(f32[5,2,16,512]{3,2,1,0:T(8,128)} %get-tuple-element.21), channel_id=1, source_target_pairs={{0,4},{4,8},{8,12},{12,16},{16,20},{20,24},{24,28},{28,32},{32,36}... | collective-permute-start | bytes 983048 | tf_op jit(solution)/shard_map/ppermute | solution.py:698
  102.8 32.2 %collective-permute-start.6 = (f32[5,2,16,512]{3,2,1,0:T(8,128)}, f32[5,2,16,512]{3,2,1,0:T(8,128)S(1)}, u32[]{:S(2)}, u32[]{:S(2)}) collective-permute-start(f32[5,2,16,512]{3,2,1,0:T(8,128)} %get-tuple-element.22), channel_id=1, source_target_pairs={{4,0},{8,4},{12,8},{16,12},{20,16},{24,20},{28,24},{32,28},{36,32}... | collective-permute-start | bytes 983048 | tf_op jit(solution)/shard_map/ppermute | solution.py:699
  107.6 8.6 %collective-permute-start.9 = (f32[5,2,8,128]{3,2,1,0:T(8,128)S(1)}, f32[5,2,8,128]{3,2,1,0:T(8,128)S(1)}, u32[]{:S(2)}, u32[]{:S(2)}) collective-permute-start(f32[5,2,8,128]{3,2,1,0:T(8,128)S(1)} %get-tuple-element.28), channel_id=1, source_target_pairs={{0,5},{1,6},{2,7},{4,9},{5,10},{6,11},{8,13},{9,14},{10,15},{12,17... | collective-permute-start | bytes 122888 | tf_op jit(solution)/shard_map/ppermute | solution.py:702
  116.2 7.7 %collective-permute-start.12 = (f32[5,2,8,128]{3,2,1,0:T(8,128)S(1)}, f32[5,2,8,128]{3,2,1,0:T(8,128)S(1)}, u32[]{:S(2)}, u32[]{:S(2)}) collective-permute-start(f32[5,2,8,128]{3,2,1,0:T(8,128)S(1)} %get-tuple-element.25), channel_id=1, source_target_pairs={{5,0},{6,1},{7,2},{9,4},{10,5},{11,6},{13,8},{14,9},{15,10},{17,12... | collective-permute-start | bytes 122888 | tf_op jit(solution)/shard_map/ppermute | solution.py:705
  123.9 11.0 %collective-permute-start.10 = (f32[5,2,8,128]{3,2,1,0:T(8,128)S(1)}, f32[5,2,8,128]{3,2,1,0:T(8,128)S(1)}, u32[]{:S(2)}, u32[]{:S(2)}) collective-permute-start(f32[5,2,8,128]{3,2,1,0:T(8,128)S(1)} %get-tuple-element.26), channel_id=1, source_target_pairs={{1,4},{2,5},{3,6},{5,8},{6,9},{7,10},{9,12},{10,13},{11,14},{13,16... | collective-permute-start | bytes 122888 | tf_op jit(solution)/shard_map/ppermute | solution.py:703
  135.0 0.7 copy-start.2
